TPU v7x, 1024 devices: a whole 4x8x16 slice. The times are simulated.
1024 devices in a mesh: band: 16 (over z), patch: 64 (over x, y, core).
Axes of the slice: x: 4, y: 8, z: 16, core: 2. Of those that a mesh axis runs over, the one named last changes fastest.
Arguments:
- grid_feat: bfloat16 [262144, 474], P(('band', 'patch')), may hold values from -6 to 6
- enc_sender: int32 [393216], P(('band', 'patch')), may hold values from 0 to 255
- enc_patch: int32 [393216, 1], P(('band', 'patch')), may hold values from 0 to 63; in each aligned block of 384 rows (0 to 383, 384 to 767, ...) at most 8 rows name the same one
- enc_node: int32 [393216], P(('band', 'patch')), may hold values from 0 to 319
- enc_geo: bfloat16 [4, 393216], P(None, ('band', 'patch')), may hold values from -6 to 6
- mesh_nodes: bfloat16 [20480, 512], P('patch'), may hold values from -6 to 6
- mesh_edge: bfloat16 [262144, 512], P(('band', 'patch')), may hold values from -6 to 6
- mesh_send: int32 [262144], P(('band', 'patch')), may hold values from 0 to 575
- mesh_recv: int32 [262144], P(('band', 'patch')), may hold values from 0 to 319
- halo_rows: int32 [64, 256], P('patch'), may hold values from 0 to 319
- grid_in: bfloat16 [474, 512], replicated, may hold values from -0.25 to 0.25
- grid_out: bfloat16 [512, 512], replicated, may hold values from -0.25 to 0.25
- geo_weight: bfloat16 [4, 512], replicated, may hold values from -3 to 3
- enc_edge_w: bfloat16 [3, 512, 512], replicated, may hold values from -0.25 to 0.25
- enc_node_w: bfloat16 [3, 512, 512], replicated, may hold values from -0.25 to 0.25
- proc_edge_w: bfloat16 [4, 512, 512], replicated, may hold values from -0.25 to 0.25
- proc_node_w: bfloat16 [3, 512, 512], replicated, may hold values from -0.25 to 0.25
Outputs:
- mesh_two: bfloat16 [20480, 512], P('patch')
- edge_out: bfloat16 [262144, 512], P(('band', 'patch'))
Inputs may be any that keep to these rules, and one draw needn't show every extreme that they name: `enc_sender`: row among the 256 grid rows of the device that holds the edge. `enc_patch`: among the 384 edge rows of one device no patch is named more than 8 times; some patch exactly 8 times. `halo_rows`: row q holds, in blocks of 4, the rows of patch q sent to patches 0, 1, ...
All inputs are finite; a program needn't handle non-finite values.
Results may differ from a plain program's by a relative error of at most 0.017.
Values may be sent and summed in bfloat16 or wider, within the bound.
A program may use at most 32 MiB of HBM per device.

v0:
```python
import jax
import jax.numpy as jnp
from jax import lax
from jax.sharding import Mesh
from jax.sharding import PartitionSpec as P

PATCH = ("patch_0", "patch_1", "patch_2")
BAND_PATCH = ("band", "patch_0", "patch_1", "patch_2")


def cut_along(value, dim, length):
    before, after = (value.shape[:dim], value.shape[dim + 1 :])
    return jnp.moveaxis(value.reshape(*before, length, -1, *after), dim, 0)


def sum_at_owner(value, axis, dim):
    pieces = cut_along(value, dim, lax.axis_size(axis))
    arrived = lax.all_to_all(pieces, axis, split_axis=0, concat_axis=0, tiled=True)
    return arrived.astype(jnp.float32).sum(axis=0)


def laid_out(pieces, dim):
    lengths = list(pieces.shape[1:])
    lengths[dim] *= pieces.shape[0]
    return jnp.moveaxis(pieces, 0, dim).reshape(lengths)


def from_everyone(value, axis):
    length = lax.axis_size(axis)
    return lax.all_to_all(
        jnp.broadcast_to(value[None], (length, *value.shape)), axis, 0, 0, tiled=True
    )


def gather_directly(value, axis, dim):
    return laid_out(from_everyone(value, axis), dim)


def exchange_in_order(pieces, axes, order):
    lengths = [lax.axis_size(a) for a in axes]
    pieces = pieces.reshape(*lengths, *pieces.shape[1:])
    for k in order:
        pieces = lax.all_to_all(pieces, axes[k], split_axis=k, concat_axis=k, tiled=True)
    return pieces.reshape(-1, *pieces.shape[len(axes) :])


def core_and_chips(value, groups, order, split_dim, concat_dim):
    length = lax.axis_size(groups[0]) * lax.axis_size(groups[1])
    pieces = cut_along(value, split_dim, length)
    return laid_out(exchange_in_order(pieces, groups, order), concat_dim)


def norm_rows(values_in):
    average = jnp.mean(values_in, axis=-1, keepdims=True)
    centred = values_in - average
    spread = jnp.mean(centred * centred, axis=-1, keepdims=True)
    return centred * lax.rsqrt(spread + 1e-05)


def network_tail(preact, out_weight):
    hidden = jax.nn.silu(preact).astype(jnp.bfloat16)
    return norm_rows(jnp.dot(hidden, out_weight, preferred_element_type=jnp.float32))


def update_rows(node_rows, running, weights):
    preact = jnp.dot(node_rows, weights[0], preferred_element_type=jnp.float32) + jnp.dot(
        running.astype(jnp.bfloat16), weights[1], preferred_element_type=jnp.float32
    )
    return (node_rows.astype(jnp.float32) + network_tail(preact, weights[2])).astype(jnp.bfloat16)


def node_update(node_rows, partial_value, weights):
    share_rows = sum_at_owner(partial_value.astype(jnp.bfloat16), "band", 0)
    row_count = share_rows.shape[0]
    first_row = lax.axis_index("band") * row_count
    own_rows = lax.dynamic_slice_in_dim(node_rows, first_row, row_count, 0)
    updated = update_rows(own_rows, share_rows, weights)
    return gather_directly(updated, "band", 0)


def per_device(
    grid_feat,
    enc_sender,
    enc_patch,
    enc_node,
    enc_geo,
    mesh_nodes,
    mesh_edge,
    mesh_send,
    mesh_recv,
    halo_rows,
    grid_in,
    grid_out,
    geo_weight,
    enc_edge_w,
    enc_node_w,
    proc_edge_w,
    proc_node_w,
):
    peer_count = lax.axis_size(PATCH)
    latent_width = mesh_nodes.shape[1]
    mesh_count = mesh_nodes.shape[0]
    edge_count = enc_sender.shape[0]
    capacity = 4 * edge_count // (3 * peer_count)
    hidden = jax.nn.silu(jnp.dot(grid_feat, grid_in, preferred_element_type=jnp.float32)).astype(
        jnp.bfloat16
    )
    grid_lat = norm_rows(jnp.dot(hidden, grid_out, preferred_element_type=jnp.float32)).astype(
        jnp.bfloat16
    )
    sender_proj = jnp.dot(grid_lat, enc_edge_w[0], preferred_element_type=jnp.float32)
    geo_term = lax.dot_general(
        enc_geo, geo_weight, (((0,), (0,)), ((), ())), preferred_element_type=jnp.float32
    )
    send_term = (sender_proj[enc_sender] + geo_term).astype(jnp.bfloat16)
    target = enc_patch[:, 0]
    onehot = (target[:, None] == jnp.arange(peer_count, dtype=jnp.int32)[None, :]).astype(jnp.int32)
    slot_index = jnp.sum((jnp.cumsum(onehot, axis=0) - 1) * onehot, axis=1)
    outbox = (
        jnp.zeros((peer_count, capacity, latent_width), jnp.bfloat16)
        .at[target, slot_index]
        .set(send_term)
    )
    addresses = (
        jnp.full((peer_count, capacity), mesh_count, jnp.int32).at[target, slot_index].set(enc_node)
    )
    recv_proj = jnp.dot(mesh_nodes, enc_edge_w[1], preferred_element_type=jnp.float32)
    sender_terms = core_and_chips(outbox, (("patch_0", "patch_1"), "patch_2"), (1, 0), 0, 0)
    places = core_and_chips(addresses, (("patch_0", "patch_1"), "patch_2"), (1, 0), 0, 0)
    preact = sender_terms.astype(jnp.float32) + recv_proj[jnp.minimum(places, mesh_count - 1)]
    messages, places = (network_tail(preact, enc_edge_w[2]), places)
    partial_value = (
        jnp.zeros((mesh_count, latent_width), jnp.float32)
        .at[places.reshape(-1)]
        .add(messages.reshape(-1, latent_width), mode="drop")
    )
    mesh_one = node_update(mesh_nodes, partial_value, enc_node_w)
    sent_proj = jnp.dot(mesh_one, proc_edge_w[1], preferred_element_type=jnp.float32).astype(
        jnp.bfloat16
    )
    recv_two = jnp.dot(mesh_one, proc_edge_w[2], preferred_element_type=jnp.float32)
    outgoing = sent_proj[halo_rows[0]].reshape(peer_count, -1, latent_width)
    ghosts = lax.all_to_all(outgoing, PATCH, split_axis=0, concat_axis=0, tiled=True)
    lookup = jnp.concatenate([sent_proj, ghosts.reshape(-1, latent_width)], axis=0)
    preact = (
        jnp.dot(mesh_edge, proc_edge_w[0], preferred_element_type=jnp.float32)
        + lookup[mesh_send].astype(jnp.float32)
        + recv_two[mesh_recv]
    )
    edge_new = mesh_edge.astype(jnp.float32) + network_tail(preact, proc_edge_w[3])
    partial_two = jnp.zeros((mesh_count, latent_width), jnp.float32).at[mesh_recv].add(edge_new)
    mesh_two = node_update(mesh_one, partial_two, proc_node_w)
    return (mesh_two, edge_new.astype(jnp.bfloat16))


def solution(mesh):
    split = Mesh(
        mesh.devices.reshape(mesh.shape["band"], 4, 8, 2), ("band", "patch_0", "patch_1", "patch_2")
    )
    placed = (
        P(BAND_PATCH, None),
        P(BAND_PATCH),
        P(BAND_PATCH, None),
        P(BAND_PATCH),
        P(None, BAND_PATCH),
        P(PATCH, None),
        P(BAND_PATCH, None),
        P(BAND_PATCH),
        P(BAND_PATCH),
        P(PATCH, None),
        P(),
        P(),
        P(),
        P(),
        P(),
        P(),
        P(),
    )
    return jax.shard_map(
        per_device,
        mesh=split,
        in_specs=placed,
        out_specs=(P(PATCH, None), P(BAND_PATCH, None)),
        check_vma=False,
    )
```

profile of v0, /device:TPU:6, one launch (start us, length us, event | category | flops | bytes accessed | tf_op | source)
XLA Modules:
  0.0 283.8 jit_solution(7744090642417990862)
XLA Ops:
  0.6 0.8 reduce.2
  1.4 0.9 reduce-window.6
  2.3 0.2 slice_reduce_fusion
  2.6 0.1 fusion.61
  2.7 0.7 fusion.76
  3.4 32.3 %scatter_fusion = s32[64,8]{0,1:T(8,128)S(1)} fusion(s32[64,8]{0,1:T(8,128)S(1)} %broadcast.230, s32[384]{0:T(512)S(1)} %fusion.76, s32[384]{0:T(512)} %param.20), kind=kCustom, calls=%fused_computation.5 | custom fusion | bytes 7680 | tf_op jit(solution)/shard_map/scatter | solution.py:125
  35.9 0.7 reshape.288
  36.6 3.2 %all-to-all-start = ((s32[2,1,256]{2,1,0:T(1,128)}), s32[2,1,256]{2,1,0:T(1,128)S(1)}, u32[]{:S(2)}, u32[]{:S(2)}) async-start(s32[2,1,256]{2,1,0:T(1,128)} %reshape.288), calls=%async_computation | async-start | bytes 4096 | tf_op jit(solution)/shard_map/all_to_all | solution.py:43
  39.9 0.7 fusion.83
  40.6 0.2 multiply_reduce_fusion.2
  40.8 0.5 copy-done.1
  41.3 0.3 fusion.24
  41.7 1.6 gather_fusion
  43.3 0.3 fusion
  43.7 20.7 %scatter_fusion.1 = bf16[64,8,512]{2,1,0:T(8,128)(2,1)S(1)} fusion(bf16[64,8,512]{2,1,0:T(8,128)(2,1)S(1)} %broadcast_in_dim.12, s32[384]{0:T(512)S(1)} %fusion.76, bf16[384,512]{1,0:T(8,128)(2,1)S(1)} %fusion), kind=kCustom, calls=%fused_computation.6 | custom fusion | bytes 1182720 | tf_op jit(solution)/shard_map/scatter | solution.py:122
  64.4 0.8 copy.31
  65.3 3.5 %all-to-all-start.2 = ((bf16[32,2,1,8,512]{4,3,0,2,1:T(8,128)(2,1)}), bf16[32,2,1,8,512]{4,3,0,2,1:T(8,128)(2,1)S(1)}, u32[]{:S(2)}, u32[]{:S(2)}) async-start(bf16[32,2,1,8,512]{4,3,0,2,1:T(8,128)(2,1)} %copy.31), calls=%async_computation.2 | async-start | bytes 1048576 | tf_op jit(solution)/shard_map/all_to_all | solution.py:43
  68.8 0.5 broadcast.341
  69.3 0.7 reduce.8
  70.0 0.7 copy.30
  70.7 16.7 %all-to-all-start.1 = ((s32[32,2,1,8]{3,1,2,0:T(2,128)}), s32[32,2,1,8]{3,1,2,0:T(2,128)S(1)}, u32[]{:S(2)}, u32[]{:S(2)}) async-start(s32[32,2,1,8]{3,1,2,0:T(2,128)} %copy.30), calls=%async_computation.1 | async-start | bytes 65536 | tf_op jit(solution)/shard_map/all_to_all | solution.py:43
  87.5 0.9 copy.32
  88.3 7.1 %all-to-all-done.1 = s32[32,2,1,8]{3,1,2,0:T(2,128)S(1)} async-done(((s32[32,2,1,8]{3,1,2,0:T(2,128)}), s32[32,2,1,8]{3,1,2,0:T(2,128)S(1)}, u32[]{:S(2)}, u32[]{:S(2)}) %all-to-all-start.1) | async-done | bytes 2080 | tf_op jit(solution)/shard_map/all_to_all | solution.py:43
  95.4 5.8 %all-to-all-start.3 = ((bf16[32,2,1,8,512]{4,3,1,2,0:T(8,128)(2,1)}), bf16[32,2,1,8,512]{4,3,1,2,0:T(8,128)(2,1)S(1)}, u32[]{:S(2)}, u32[]{:S(2)}) async-start(bf16[32,2,1,8,512]{4,3,1,2,0:T(8,128)(2,1)} %copy.32), calls=%async_computation.3 | async-start | bytes 1048576 | tf_op jit(solution)/shard_map/all_to_all | solution.py:43
  101.2 1.3 fusion.22
  102.7 1.6 gather_fusion.1
  104.3 0.1 reshape_reshape_reshape.3
  104.4 11.6 %all-to-all-done.3 = bf16[32,2,1,8,512]{4,3,1,2,0:T(8,128)(2,1)S(1)} async-done(((bf16[32,2,1,8,512]{4,3,1,2,0:T(8,128)(2,1)}), bf16[32,2,1,8,512]{4,3,1,2,0:T(8,128)(2,1)S(1)}, u32[]{:S(2)}, u32[]{:S(2)}) %all-to-all-start.3) | async-done | bytes 524320 | tf_op jit(solution)/shard_map/all_to_all | solution.py:43
  116.0 0.3 multiply_convert_fusion
  116.3 1.6 fusion.84
  117.9 0.3 multiply_reduce_fusion
  118.2 3.9 %scatter_custom_fusion.2 = f32[320,512]{1,0:T(8,128)S(1)} fusion(s32[512]{0:T(512)S(1)} %bitcast.125, f32[64,8,512]{2,1,0:T(8,128)S(1)} %get-tuple-element.5, f32[64,8]{1,0:T(8,128)S(1)} %add_rsqrt_fusion, f32[64,8]{1,0:T(8,128)S(1)} %broadcast_multiply_fusion, f32[]{:T(128)} %constant.29.clone.1), kind=kCustom, calls=%fused_computation.16 | custom fusion | flops 786432 | bytes 1769476 | tf_op jit(solution)/shard_map/scatter-add | solution.py:135
  122.2 0.8 reshape.199
  123.0 12.2 %all-to-all-start.4 = ((bf16[16,20,512]{2,1,0:T(8,128)(2,1)}), bf16[16,20,512]{2,1,0:T(8,128)(2,1)S(1)}, u32[]{:S(2)}, u32[]{:S(2)}) async-start(bf16[16,20,512]{2,1,0:T(8,128)(2,1)} %reshape.199), calls=%async_computation.4 | async-start | bytes 786432 | tf_op jit(solution)/shard_map/all_to_all | solution.py:18
  135.2 1.2 fusion.26
  136.5 18.4 %all-to-all-done.4 = bf16[16,20,512]{2,1,0:T(8,128)(2,1)S(1)} async-done(((bf16[16,20,512]{2,1,0:T(8,128)(2,1)}), bf16[16,20,512]{2,1,0:T(8,128)(2,1)S(1)}, u32[]{:S(2)}, u32[]{:S(2)}) %all-to-all-start.4) | async-done | bytes 327712 | tf_op jit(solution)/shard_map/all_to_all | solution.py:18
  155.0 0.5 fusion.85
  155.5 0.2 multiply_reduce_fusion.4
  155.7 0.8 add_convert_fusion.1
  156.5 0.8 broadcast_in_dim.14
  157.3 6.7 %all-to-all-start.5 = ((bf16[16,20,512]{2,1,0:T(8,128)(2,1)}), bf16[16,20,512]{2,1,0:T(8,128)(2,1)S(1)}, u32[]{:S(2)}, u32[]{:S(2)}) async-start(bf16[16,20,512]{2,1,0:T(8,128)(2,1)} %broadcast_in_dim.14), calls=%async_computation.5 | async-start | bytes 786432 | tf_op jit(solution)/shard_map/all_to_all | solution.py:30
  164.0 20.4 %all-to-all-done.5 = bf16[16,20,512]{2,1,0:T(8,128)(2,1)S(1)} async-done(((bf16[16,20,512]{2,1,0:T(8,128)(2,1)}), bf16[16,20,512]{2,1,0:T(8,128)(2,1)S(1)}, u32[]{:S(2)}, u32[]{:S(2)}) %all-to-all-start.5) | async-done | bytes 327712 | tf_op jit(solution)/shard_map/all_to_all | solution.py:30
  184.5 1.4 convolution_convert_fusion
  185.9 1.2 gather_fusion.2
  187.0 0.8 reshape.201
  187.8 13.8 %all-to-all-start.6 = ((bf16[64,4,512]{2,1,0:T(4,128)(2,1)}), bf16[64,4,512]{2,1,0:T(4,128)(2,1)S(1)}, u32[]{:S(2)}, u32[]{:S(2)}) async-start(bf16[64,4,512]{2,1,0:T(4,128)(2,1)} %reshape.201), calls=%async_computation.6 | async-start | bytes 524288 | tf_op jit(solution)/shard_map/all_to_all | solution.py:143
  201.7 1.4 fusion.11
  203.1 1.0 gather_fusion.4
  204.0 9.1 %all-to-all-done.6 = bf16[64,4,512]{2,1,0:T(4,128)(2,1)S(1)} async-done(((bf16[64,4,512]{2,1,0:T(4,128)(2,1)}), bf16[64,4,512]{2,1,0:T(4,128)(2,1)S(1)}, u32[]{:S(2)}, u32[]{:S(2)}) %all-to-all-start.6) | async-done | bytes 262176 | tf_op jit(solution)/shard_map/all_to_all | solution.py:143
  213.3 1.2 gather_fusion.3
  214.5 1.9 fusion.88
  216.4 0.2 multiply_reduce_fusion.1
  216.6 2.4 scatter_custom_fusion.3
  219.0 0.8 reshape.203
  219.8 6.2 %all-to-all-start.7 = ((bf16[16,20,512]{2,1,0:T(8,128)(2,1)}), bf16[16,20,512]{2,1,0:T(8,128)(2,1)S(1)}, u32[]{:S(2)}, u32[]{:S(2)}) async-start(bf16[16,20,512]{2,1,0:T(8,128)(2,1)} %reshape.203), calls=%async_computation.7 | async-start | bytes 786432 | tf_op jit(solution)/shard_map/all_to_all | solution.py:18
  226.0 1.2 fusion.15
  227.2 23.0 %all-to-all-done.7 = bf16[16,20,512]{2,1,0:T(8,128)(2,1)S(1)} async-done(((bf16[16,20,512]{2,1,0:T(8,128)(2,1)}), bf16[16,20,512]{2,1,0:T(8,128)(2,1)S(1)}, u32[]{:S(2)}, u32[]{:S(2)}) %all-to-all-start.7) | async-done | bytes 327712 | tf_op jit(solution)/shard_map/all_to_all | solution.py:18
  250.4 1.7 fusion.91
  252.0 0.2 multiply_reduce_fusion.3
  252.3 0.8 broadcast_in_dim.17
  253.1 5.8 %all-to-all-start.8 = ((bf16[16,20,512]{2,1,0:T(8,128)(2,1)}), bf16[16,20,512]{2,1,0:T(8,128)(2,1)S(1)}, u32[]{:S(2)}, u32[]{:S(2)}) async-start(bf16[16,20,512]{2,1,0:T(8,128)(2,1)} %broadcast_in_dim.17), calls=%async_computation.8 | async-start | bytes 786432 | tf_op jit(solution)/shard_map/all_to_all | solution.py:30
  258.9 0.9 fusion.52
  259.8 23.3 %all-to-all-done.8 = bf16[16,20,512]{2,1,0:T(8,128)(2,1)S(1)} async-done(((bf16[16,20,512]{2,1,0:T(8,128)(2,1)}), bf16[16,20,512]{2,1,0:T(8,128)(2,1)S(1)}, u32[]{:S(2)}, u32[]{:S(2)}) %all-to-all-start.8) | async-done | bytes 327712 | tf_op jit(solution)/shard_map/all_to_all | solution.py:30
  283.0 0.8 reshape.204
  (63 shorter events, 1.1 us)
Async XLA Ops:
  0.6 39.2 %copy-start = (bf16[512,512]{1,0:T(8,128)(2,1)S(1)}, bf16[512,512]{1,0:T(8,128)(2,1)}, u32[]{:S(2)}) copy-start(bf16[512,512]{1,0:T(8,128)(2,1)} %param.28) | copy-start | bytes 1572868
  3.4 36.4 %copy-start.10 = (bf16[474,512]{1,0:T(8,128)(2,1)S(1)}, bf16[474,512]{1,0:T(8,128)(2,1)}, u32[]{:S(2)}) copy-start(bf16[474,512]{1,0:T(8,128)(2,1)} %param.27) | copy-start | bytes 1456132
  3.4 36.4 %copy-start.11 = (bf16[256,474]{0,1:T(8,128)(2,1)S(1)}, bf16[256,474]{0,1:T(8,128)(2,1)}, u32[]{:S(2)}) copy-start(bf16[256,474]{0,1:T(8,128)(2,1)} %param.17) | copy-start | bytes 728068
  36.6 28.7 %all-to-all-start = ((s32[2,1,256]{2,1,0:T(1,128)}), s32[2,1,256]{2,1,0:T(1,128)S(1)}, u32[]{:S(2)}, u32[]{:S(2)}) async-start(s32[2,1,256]{2,1,0:T(1,128)} %reshape.288), calls=%async_computation | async-start | bytes 4096 | tf_op jit(solution)/shard_map/all_to_all | solution.py:43
  39.9 0.9 copy-start.6
  39.9 1.4 copy-start.1
  41.6 1.7 copy-start.4
  41.7 1.7 copy-start.5
  65.3 5.5 %all-to-all-start.2 = ((bf16[32,2,1,8,512]{4,3,0,2,1:T(8,128)(2,1)}), bf16[32,2,1,8,512]{4,3,0,2,1:T(8,128)(2,1)S(1)}, u32[]{:S(2)}, u32[]{:S(2)}) async-start(bf16[32,2,1,8,512]{4,3,0,2,1:T(8,128)(2,1)} %copy.31), calls=%async_computation.2 | async-start | bytes 1048576 | tf_op jit(solution)/shard_map/all_to_all | solution.py:43
  70.7 24.7 %all-to-all-start.1 = ((s32[32,2,1,8]{3,1,2,0:T(2,128)}), s32[32,2,1,8]{3,1,2,0:T(2,128)S(1)}, u32[]{:S(2)}, u32[]{:S(2)}) async-start(s32[32,2,1,8]{3,1,2,0:T(2,128)} %copy.30), calls=%async_computation.1 | async-start | bytes 65536 | tf_op jit(solution)/shard_map/all_to_all | solution.py:43
  95.4 20.6 %all-to-all-start.3 = ((bf16[32,2,1,8,512]{4,3,1,2,0:T(8,128)(2,1)}), bf16[32,2,1,8,512]{4,3,1,2,0:T(8,128)(2,1)S(1)}, u32[]{:S(2)}, u32[]{:S(2)}) async-start(bf16[32,2,1,8,512]{4,3,1,2,0:T(8,128)(2,1)} %copy.32), calls=%async_computation.3 | async-start | bytes 1048576 | tf_op jit(solution)/shard_map/all_to_all | solution.py:43
  122.2 32.8 %copy-start.3 = (bf16[3,512,512]{2,1,0:T(8,128)(2,1)S(1)}, bf16[3,512,512]{2,1,0:T(8,128)(2,1)}, u32[]{:S(2)}) copy-start(bf16[3,512,512]{2,1,0:T(8,128)(2,1)} %param.31) | copy-start | bytes 4718596
  123.0 31.9 %all-to-all-start.4 = ((bf16[16,20,512]{2,1,0:T(8,128)(2,1)}), bf16[16,20,512]{2,1,0:T(8,128)(2,1)S(1)}, u32[]{:S(2)}, u32[]{:S(2)}) async-start(bf16[16,20,512]{2,1,0:T(8,128)(2,1)} %reshape.199), calls=%async_computation.4 | async-start | bytes 786432 | tf_op jit(solution)/shard_map/all_to_all | solution.py:18
  136.5 27.5 %copy-start.7 = (s32[1,256]{1,0:T(1,128)S(1)}, s32[1,256]{1,0:T(1,128)}, u32[]{:S(2)}) copy-start(s32[1,256]{1,0:T(1,128)} %param.26) | copy-start | bytes 3076
  136.5 27.5 %copy-start.8 = (s32[256]{0:T(256)S(1)}, s32[256]{0:T(256)}, u32[]{:S(2)}) copy-start(s32[256]{0:T(256)} %param.24) | copy-start | bytes 3076
  157.3 27.1 %all-to-all-start.5 = ((bf16[16,20,512]{2,1,0:T(8,128)(2,1)}), bf16[16,20,512]{2,1,0:T(8,128)(2,1)S(1)}, u32[]{:S(2)}, u32[]{:S(2)}) async-start(bf16[16,20,512]{2,1,0:T(8,128)(2,1)} %broadcast_in_dim.14), calls=%async_computation.5 | async-start | bytes 786432 | tf_op jit(solution)/shard_map/all_to_all | solution.py:30
  185.9 15.8 %copy-start.9 = (s32[256]{0:T(256)S(1)}, s32[256]{0:T(256)}, u32[]{:S(2)}) copy-start(s32[256]{0:T(256)} %param.25) | copy-start | bytes 3076
  187.8 25.4 %all-to-all-start.6 = ((bf16[64,4,512]{2,1,0:T(4,128)(2,1)}), bf16[64,4,512]{2,1,0:T(4,128)(2,1)S(1)}, u32[]{:S(2)}, u32[]{:S(2)}) async-start(bf16[64,4,512]{2,1,0:T(4,128)(2,1)} %reshape.201), calls=%async_computation.6 | async-start | bytes 524288 | tf_op jit(solution)/shard_map/all_to_all | solution.py:143
  213.3 1.2 copy-start.2
  219.8 30.4 %all-to-all-start.7 = ((bf16[16,20,512]{2,1,0:T(8,128)(2,1)}), bf16[16,20,512]{2,1,0:T(8,128)(2,1)S(1)}, u32[]{:S(2)}, u32[]{:S(2)}) async-start(bf16[16,20,512]{2,1,0:T(8,128)(2,1)} %reshape.203), calls=%async_computation.7 | async-start | bytes 786432 | tf_op jit(solution)/shard_map/all_to_all | solution.py:18
  253.1 29.9 %all-to-all-start.8 = ((bf16[16,20,512]{2,1,0:T(8,128)(2,1)}), bf16[16,20,512]{2,1,0:T(8,128)(2,1)S(1)}, u32[]{:S(2)}, u32[]{:S(2)}) async-start(bf16[16,20,512]{2,1,0:T(8,128)(2,1)} %broadcast_in_dim.17), calls=%async_computation.8 | async-start | bytes 786432 | tf_op jit(solution)/shard_map/all_to_all | solution.py:30
where the time goes:
time: 286 us; the launch traced here: 284 us
  waiting for transfers between devices  113 us (40%)
  starting transfers between devices  73.9 us (26%)
  local copies, waits for them, and re-layouts  69.2 us (24%)
  matrix products  13.4 us (5%)
  other arithmetic  13.1 us (5%)
    all_to_all x2, waiting for transfers between devices, from_everyone(): lax.all_to_all(jnp.broadcast_to(value[None], (length, *value.shape)), axi...  43.6 us
    all_to_all x2, waiting for transfers between devices, sum_at_owner(): lax.all_to_all(pieces, axis, split_axis=0, concat_axis=0, tiled=True)  41.5 us
    scatter x2, local copies, waits for them, and re-layouts, per_device(): jnp.full((peer_count, capacity), mesh_count, jnp.int32)  32.4 us
    all_to_all x4, starting transfers between devices, exchange_in_order(): lax.all_to_all(pieces, axes[k], split_axis=k, concat_axis=k, tiled=True)  29.2 us
    scatter x1, local copies, waits for them, and re-layouts, per_device(): outbox = jnp.zeros((peer_count, capacity, latent_width), jnp.bfloat16).at...  20.7 us
    all_to_all x4, waiting for transfers between devices, exchange_in_order(): lax.all_to_all(pieces, axes[k], split_axis=k, concat_axis=k, tiled=True)  18.7 us
    all_to_all x2, starting transfers between devices, sum_at_owner(): lax.all_to_all(pieces, axis, split_axis=0, concat_axis=0, tiled=True)  18.4 us
    all_to_all x1, starting transfers between devices, per_device(): lax.all_to_all(outgoing, PATCH, split_axis=0, concat_axis=0, tiled=True)  13.8 us
  transfers between devices with their start and end apart: 9, of which 7 were waited for; matrix products, arithmetic and copies ran while one was open for 13% of the time, Pallas kernels for 0%

commit v1 on v0

--- a/solution.py
+++ b/solution.py
@@ -116,23 +116,23 @@
     target = enc_patch[:, 0]
     onehot = (target[:, None] == jnp.arange(peer_count, dtype=jnp.int32)[None, :]).astype(jnp.int32)
     slot_index = jnp.sum((jnp.cumsum(onehot, axis=0) - 1) * onehot, axis=1)
-    outbox = (
-        jnp.zeros((peer_count, capacity, latent_width), jnp.bfloat16)
-        .at[target, slot_index]
-        .set(send_term)
-    )
-    addresses = (
-        jnp.full((peer_count, capacity), mesh_count, jnp.int32).at[target, slot_index].set(enc_node)
-    )
+    slots = peer_count * capacity
+    chosen = (target * capacity + slot_index)[None, :] == jnp.arange(slots, dtype=jnp.int32)[:, None]
+    outbox = jnp.dot(
+        chosen.astype(jnp.bfloat16), send_term, preferred_element_type=jnp.float32
+    ).astype(jnp.bfloat16).reshape(peer_count, capacity, latent_width)
+    addresses = jnp.sum(jnp.where(chosen, enc_node[None, :] - mesh_count, 0), axis=1) + mesh_count
+    addresses = addresses.reshape(peer_count, capacity)
     recv_proj = jnp.dot(mesh_nodes, enc_edge_w[1], preferred_element_type=jnp.float32)
     sender_terms = core_and_chips(outbox, (("patch_0", "patch_1"), "patch_2"), (1, 0), 0, 0)
     places = core_and_chips(addresses, (("patch_0", "patch_1"), "patch_2"), (1, 0), 0, 0)
     preact = sender_terms.astype(jnp.float32) + recv_proj[jnp.minimum(places, mesh_count - 1)]
     messages, places = (network_tail(preact, enc_edge_w[2]), places)
-    partial_value = (
-        jnp.zeros((mesh_count, latent_width), jnp.float32)
-        .at[places.reshape(-1)]
-        .add(messages.reshape(-1, latent_width), mode="drop")
+    landing = jnp.arange(mesh_count, dtype=jnp.int32)[:, None] == places.reshape(-1)[None, :]
+    partial_value = jnp.dot(
+        landing.astype(jnp.bfloat16),
+        messages.reshape(-1, latent_width).astype(jnp.bfloat16),
+        preferred_element_type=jnp.float32,
     )
     mesh_one = node_update(mesh_nodes, partial_value, enc_node_w)
     sent_proj = jnp.dot(mesh_one, proc_edge_w[1], preferred_element_type=jnp.float32).astype(

time: 286 us -> 232 us (0.81)
  local copies, waits for them, and re-layouts: 69.2 us -> 16.3 us
  other arithmetic: 13.1 us -> 9.95 us
  matrix products: 13.4 us -> 16.3 us
    scatter x3 -> x0, local copies, waits for them, and re-layouts: 53.2 us -> none  [the longest x2 32.4 us: per_device(): jnp.full((peer_count, capacity), mesh_count, jnp.int32)]
    scatter-add x1 -> x0, other arithmetic: 3.94 us -> none  [per_device(): partial_value = jnp.zeros((mesh_count, latent_width), jnp.float32).at[pla...]
  transfers between devices with their start and end apart: 9 -> 9, of which waited for: 7 -> 7; matrix products, arithmetic and copies ran while one was open for 13% -> 8% of each run, Pallas kernels for 0% -> 0%
where the time goes in v1:
time: 232 us; the launch traced here: 231 us
  waiting for transfers between devices  113 us (49%)
  starting transfers between devices  73.8 us (32%)
  local copies, waits for them, and re-layouts  16.3 us (7%)
  matrix products  16.3 us (7%)
  other arithmetic  9.95 us (4%)
    all_to_all x2, waiting for transfers between devices, from_everyone(): lax.all_to_all(jnp.broadcast_to(value[None], (length, *value.shape)), axi...  43.6 us
    all_to_all x2, waiting for transfers between devices, sum_at_owner(): lax.all_to_all(pieces, axis, split_axis=0, concat_axis=0, tiled=True)  41.8 us
    all_to_all x4, starting transfers between devices, exchange_in_order(): lax.all_to_all(pieces, axes[k], split_axis=k, concat_axis=k, tiled=True)  29.3 us
    all_to_all x4, waiting for transfers between devices, exchange_in_order(): lax.all_to_all(pieces, axes[k], split_axis=k, concat_axis=k, tiled=True)  18.7 us
    all_to_all x2, starting transfers between devices, sum_at_owner(): lax.all_to_all(pieces, axis, split_axis=0, concat_axis=0, tiled=True)  18.4 us
    all_to_all x1, starting transfers between devices, per_device(): lax.all_to_all(outgoing, PATCH, split_axis=0, concat_axis=0, tiled=True)  13.6 us
    all_to_all x2, starting transfers between devices, from_everyone(): lax.all_to_all(jnp.broadcast_to(value[None], (length, *value.shape)), axi...  12.5 us
    all_to_all x1, waiting for transfers between devices, per_device(): lax.all_to_all(outgoing, PATCH, split_axis=0, concat_axis=0, tiled=True)  9.13 us
  transfers between devices with their start and end apart: 9, of which 7 were waited for; matrix products, arithmetic and copies ran while one was open for 8% of the time, Pallas kernels for 0%

profile of v1, /device:TPU:6, one launch (start us, length us, event | category | flops | bytes accessed | tf_op | source)
XLA Modules:
  0.0 230.7 jit_solution(15790453864397781699)
XLA Ops:
  0.6 0.8 reduce.2
  1.4 0.9 reduce-window.6
  2.3 0.2 slice_reduce_fusion
  2.6 0.1 fusion.60
  2.7 0.7 multiply_add_fusion.2
  3.4 0.2 select_reduce_fusion
  3.6 0.1 add.167
  3.8 0.7 reshape.245
  4.4 3.2 %all-to-all-start = ((s32[2,1,256]{2,1,0:T(1,128)}), s32[2,1,256]{2,1,0:T(1,128)S(1)}, u32[]{:S(2)}, u32[]{:S(2)}) async-start(s32[2,1,256]{2,1,0:T(1,128)} %reshape.245), calls=%async_computation | async-start | bytes 4096 | tf_op jit(solution)/shard_map/all_to_all | solution.py:43
  7.6 0.7 compare_select_fusion.2
  8.4 1.9 fusion.80
  10.3 0.2 multiply_reduce_fusion.2
  10.5 0.3 fusion.22
  10.9 2.2 gather_fusion
  13.2 1.8 convolution_convert_fusion
  15.0 0.8 copy.29
  15.8 3.5 %all-to-all-start.2 = ((bf16[32,2,1,8,512]{4,3,0,2,1:T(8,128)(2,1)}), bf16[32,2,1,8,512]{4,3,0,2,1:T(8,128)(2,1)S(1)}, u32[]{:S(2)}, u32[]{:S(2)}) async-start(bf16[32,2,1,8,512]{4,3,0,2,1:T(8,128)(2,1)} %copy.29), calls=%async_computation.2 | async-start | bytes 1048576 | tf_op jit(solution)/shard_map/all_to_all | solution.py:43
  19.3 0.5 broadcast.259
  19.8 0.7 reduce.6
  20.6 0.7 copy.28
  21.3 16.8 %all-to-all-start.1 = ((s32[32,2,1,8]{3,1,2,0:T(2,128)}), s32[32,2,1,8]{3,1,2,0:T(2,128)S(1)}, u32[]{:S(2)}, u32[]{:S(2)}) async-start(s32[32,2,1,8]{3,1,2,0:T(2,128)} %copy.28), calls=%async_computation.1 | async-start | bytes 65536 | tf_op jit(solution)/shard_map/all_to_all | solution.py:43
  38.1 0.9 copy.30
  38.9 7.1 %all-to-all-done.1 = s32[32,2,1,8]{3,1,2,0:T(2,128)S(1)} async-done(((s32[32,2,1,8]{3,1,2,0:T(2,128)}), s32[32,2,1,8]{3,1,2,0:T(2,128)S(1)}, u32[]{:S(2)}, u32[]{:S(2)}) %all-to-all-start.1) | async-done | bytes 2080 | tf_op jit(solution)/shard_map/all_to_all | solution.py:43
  46.0 5.8 %all-to-all-start.3 = ((bf16[32,2,1,8,512]{4,3,1,2,0:T(8,128)(2,1)}), bf16[32,2,1,8,512]{4,3,1,2,0:T(8,128)(2,1)S(1)}, u32[]{:S(2)}, u32[]{:S(2)}) async-start(bf16[32,2,1,8,512]{4,3,1,2,0:T(8,128)(2,1)} %copy.30), calls=%async_computation.3 | async-start | bytes 1048576 | tf_op jit(solution)/shard_map/all_to_all | solution.py:43
  51.8 1.3 fusion.20
  53.3 1.6 gather_fusion.1
  54.9 0.1 eq.62
  55.0 11.6 %all-to-all-done.3 = bf16[32,2,1,8,512]{4,3,1,2,0:T(8,128)(2,1)S(1)} async-done(((bf16[32,2,1,8,512]{4,3,1,2,0:T(8,128)(2,1)}), bf16[32,2,1,8,512]{4,3,1,2,0:T(8,128)(2,1)S(1)}, u32[]{:S(2)}, u32[]{:S(2)}) %all-to-all-start.3) | async-done | bytes 524320 | tf_op jit(solution)/shard_map/all_to_all | solution.py:43
  66.6 0.3 multiply_convert_fusion.1
  66.9 1.6 fusion.81
  68.5 0.3 multiply_reduce_fusion
  68.8 0.4 convolution_convert_fusion.2
  69.3 0.8 reshape.179
  70.1 12.2 %all-to-all-start.4 = ((bf16[16,20,512]{2,1,0:T(8,128)(2,1)}), bf16[16,20,512]{2,1,0:T(8,128)(2,1)S(1)}, u32[]{:S(2)}, u32[]{:S(2)}) async-start(bf16[16,20,512]{2,1,0:T(8,128)(2,1)} %reshape.179), calls=%async_computation.4 | async-start | bytes 786432 | tf_op jit(solution)/shard_map/all_to_all | solution.py:18
  82.3 0.9 fusion.24
  83.3 18.7 %all-to-all-done.4 = bf16[16,20,512]{2,1,0:T(8,128)(2,1)S(1)} async-done(((bf16[16,20,512]{2,1,0:T(8,128)(2,1)}), bf16[16,20,512]{2,1,0:T(8,128)(2,1)S(1)}, u32[]{:S(2)}, u32[]{:S(2)}) %all-to-all-start.4) | async-done | bytes 327712 | tf_op jit(solution)/shard_map/all_to_all | solution.py:18
  102.0 0.5 fusion.82
  102.5 0.2 multiply_reduce_fusion.4
  102.7 0.8 add_convert_fusion.1
  103.6 0.8 broadcast_in_dim.27
  104.3 6.7 %all-to-all-start.5 = ((bf16[16,20,512]{2,1,0:T(8,128)(2,1)}), bf16[16,20,512]{2,1,0:T(8,128)(2,1)S(1)}, u32[]{:S(2)}, u32[]{:S(2)}) async-start(bf16[16,20,512]{2,1,0:T(8,128)(2,1)} %broadcast_in_dim.27), calls=%async_computation.5 | async-start | bytes 786432 | tf_op jit(solution)/shard_map/all_to_all | solution.py:30
  111.1 20.4 %all-to-all-done.5 = bf16[16,20,512]{2,1,0:T(8,128)(2,1)S(1)} async-done(((bf16[16,20,512]{2,1,0:T(8,128)(2,1)}), bf16[16,20,512]{2,1,0:T(8,128)(2,1)S(1)}, u32[]{:S(2)}, u32[]{:S(2)}) %all-to-all-start.5) | async-done | bytes 327712 | tf_op jit(solution)/shard_map/all_to_all | solution.py:30
  131.5 1.4 convolution_convert_fusion.1
  132.9 1.2 gather_fusion.2
  134.1 0.8 reshape.181
  134.9 13.6 %all-to-all-start.6 = ((bf16[64,4,512]{2,1,0:T(4,128)(2,1)}), bf16[64,4,512]{2,1,0:T(4,128)(2,1)S(1)}, u32[]{:S(2)}, u32[]{:S(2)}) async-start(bf16[64,4,512]{2,1,0:T(4,128)(2,1)} %reshape.181), calls=%async_computation.6 | async-start | bytes 524288 | tf_op jit(solution)/shard_map/all_to_all | solution.py:143
  148.6 1.4 fusion.9
  149.9 1.0 gather_fusion.4
  150.9 9.1 %all-to-all-done.6 = bf16[64,4,512]{2,1,0:T(4,128)(2,1)S(1)} async-done(((bf16[64,4,512]{2,1,0:T(4,128)(2,1)}), bf16[64,4,512]{2,1,0:T(4,128)(2,1)S(1)}, u32[]{:S(2)}, u32[]{:S(2)}) %all-to-all-start.6) | async-done | bytes 262176 | tf_op jit(solution)/shard_map/all_to_all | solution.py:143
  160.2 1.2 gather_fusion.3
  161.3 1.9 fusion.85
  163.2 0.2 multiply_reduce_fusion.1
  163.4 2.4 %scatter_custom_fusion = f32[320,512]{1,0:T(8,128)S(1)} fusion(s32[256]{0:T(256)S(1)} %compare_select_fusion.4, f32[]{:T(128)} %constant.62.clone.1, bf16[256,512]{1,0:T(8,128)(2,1)S(1)} %copy-done.2, f32[256,512]{1,0:T(8,128)S(1)} %get-tuple-element.9, f32[256]{0:T(256)S(1)} %add_rsqrt_fusion.1, f32[256]{0:T(256)S(1)} %broadcast_multiply_fusion.1), kind=kCustom, calls=%fused_computation.68 | custom fusion | flops 655360 | bytes 1443844 | tf_op jit(solution)/shard_map/scatter-add | solution.py:151
  165.9 0.8 reshape.183
  166.7 6.2 %all-to-all-start.7 = ((bf16[16,20,512]{2,1,0:T(8,128)(2,1)}), bf16[16,20,512]{2,1,0:T(8,128)(2,1)S(1)}, u32[]{:S(2)}, u32[]{:S(2)}) async-start(bf16[16,20,512]{2,1,0:T(8,128)(2,1)} %reshape.183), calls=%async_computation.7 | async-start | bytes 786432 | tf_op jit(solution)/shard_map/all_to_all | solution.py:18
  172.9 1.2 fusion.13
  174.1 23.0 %all-to-all-done.7 = bf16[16,20,512]{2,1,0:T(8,128)(2,1)S(1)} async-done(((bf16[16,20,512]{2,1,0:T(8,128)(2,1)}), bf16[16,20,512]{2,1,0:T(8,128)(2,1)S(1)}, u32[]{:S(2)}, u32[]{:S(2)}) %all-to-all-start.7) | async-done | bytes 327712 | tf_op jit(solution)/shard_map/all_to_all | solution.py:18
  197.2 1.7 fusion.88
  198.9 0.2 multiply_reduce_fusion.3
  199.2 0.8 broadcast_in_dim.31
  200.0 5.8 %all-to-all-start.8 = ((bf16[16,20,512]{2,1,0:T(8,128)(2,1)}), bf16[16,20,512]{2,1,0:T(8,128)(2,1)S(1)}, u32[]{:S(2)}, u32[]{:S(2)}) async-start(bf16[16,20,512]{2,1,0:T(8,128)(2,1)} %broadcast_in_dim.31), calls=%async_computation.8 | async-start | bytes 786432 | tf_op jit(solution)/shard_map/all_to_all | solution.py:30
  205.8 0.9 fusion.51
  206.6 23.3 %all-to-all-done.8 = bf16[16,20,512]{2,1,0:T(8,128)(2,1)S(1)} async-done(((bf16[16,20,512]{2,1,0:T(8,128)(2,1)}), bf16[16,20,512]{2,1,0:T(8,128)(2,1)S(1)}, u32[]{:S(2)}, u32[]{:S(2)}) %all-to-all-start.8) | async-done | bytes 327712 | tf_op jit(solution)/shard_map/all_to_all | solution.py:30
  229.9 0.8 reshape.184
  (53 shorter events, 0.9 us)
Async XLA Ops:
  0.6 7.7 %copy-start = (bf16[512,512]{1,0:T(8,128)(2,1)S(1)}, bf16[512,512]{1,0:T(8,128)(2,1)}, u32[]{:S(2)}) copy-start(bf16[512,512]{1,0:T(8,128)(2,1)} %param.28) | copy-start | bytes 1572868
  4.4 11.4 %all-to-all-start = ((s32[2,1,256]{2,1,0:T(1,128)}), s32[2,1,256]{2,1,0:T(1,128)S(1)}, u32[]{:S(2)}, u32[]{:S(2)}) async-start(s32[2,1,256]{2,1,0:T(1,128)} %reshape.245), calls=%async_computation | async-start | bytes 4096 | tf_op jit(solution)/shard_map/all_to_all | solution.py:43
  8.3 2.2 copy-start.1
  10.9 2.3 copy-start.7
  10.9 2.3 copy-start.8
  15.8 5.5 %all-to-all-start.2 = ((bf16[32,2,1,8,512]{4,3,0,2,1:T(8,128)(2,1)}), bf16[32,2,1,8,512]{4,3,0,2,1:T(8,128)(2,1)S(1)}, u32[]{:S(2)}, u32[]{:S(2)}) async-start(bf16[32,2,1,8,512]{4,3,0,2,1:T(8,128)(2,1)} %copy.29), calls=%async_computation.2 | async-start | bytes 1048576 | tf_op jit(solution)/shard_map/all_to_all | solution.py:43
  21.3 24.7 %all-to-all-start.1 = ((s32[32,2,1,8]{3,1,2,0:T(2,128)}), s32[32,2,1,8]{3,1,2,0:T(2,128)S(1)}, u32[]{:S(2)}, u32[]{:S(2)}) async-start(s32[32,2,1,8]{3,1,2,0:T(2,128)} %copy.28), calls=%async_computation.1 | async-start | bytes 65536 | tf_op jit(solution)/shard_map/all_to_all | solution.py:43
  46.0 20.6 %all-to-all-start.3 = ((bf16[32,2,1,8,512]{4,3,1,2,0:T(8,128)(2,1)}), bf16[32,2,1,8,512]{4,3,1,2,0:T(8,128)(2,1)S(1)}, u32[]{:S(2)}, u32[]{:S(2)}) async-start(bf16[32,2,1,8,512]{4,3,1,2,0:T(8,128)(2,1)} %copy.30), calls=%async_computation.3 | async-start | bytes 1048576 | tf_op jit(solution)/shard_map/all_to_all | solution.py:43
  68.8 13.5 %copy-start.3 = (bf16[3,512,512]{2,1,0:T(8,128)(2,1)S(1)}, bf16[3,512,512]{2,1,0:T(8,128)(2,1)}, u32[]{:S(2)}) copy-start(bf16[3,512,512]{2,1,0:T(8,128)(2,1)} %param.31) | copy-start | bytes 4718596
  70.1 31.9 %all-to-all-start.4 = ((bf16[16,20,512]{2,1,0:T(8,128)(2,1)}), bf16[16,20,512]{2,1,0:T(8,128)(2,1)S(1)}, u32[]{:S(2)}, u32[]{:S(2)}) async-start(bf16[16,20,512]{2,1,0:T(8,128)(2,1)} %reshape.179), calls=%async_computation.4 | async-start | bytes 786432 | tf_op jit(solution)/shard_map/all_to_all | solution.py:18
  83.3 27.8 %copy-start.4 = (s32[1,256]{1,0:T(1,128)S(1)}, s32[1,256]{1,0:T(1,128)}, u32[]{:S(2)}) copy-start(s32[1,256]{1,0:T(1,128)} %param.26) | copy-start | bytes 3076
  83.3 27.8 %copy-start.5 = (s32[256]{0:T(256)S(1)}, s32[256]{0:T(256)}, u32[]{:S(2)}) copy-start(s32[256]{0:T(256)} %param.25) | copy-start | bytes 3076
  104.3 27.1 %all-to-all-start.5 = ((bf16[16,20,512]{2,1,0:T(8,128)(2,1)}), bf16[16,20,512]{2,1,0:T(8,128)(2,1)S(1)}, u32[]{:S(2)}, u32[]{:S(2)}) async-start(bf16[16,20,512]{2,1,0:T(8,128)(2,1)} %broadcast_in_dim.27), calls=%async_computation.5 | async-start | bytes 786432 | tf_op jit(solution)/shard_map/all_to_all | solution.py:30
  132.9 15.6 %copy-start.6 = (s32[256]{0:T(256)S(1)}, s32[256]{0:T(256)}, u32[]{:S(2)}) copy-start(s32[256]{0:T(256)} %param.24) | copy-start | bytes 3076
  134.9 25.2 %all-to-all-start.6 = ((bf16[64,4,512]{2,1,0:T(4,128)(2,1)}), bf16[64,4,512]{2,1,0:T(4,128)(2,1)S(1)}, u32[]{:S(2)}, u32[]{:S(2)}) async-start(bf16[64,4,512]{2,1,0:T(4,128)(2,1)} %reshape.181), calls=%async_computation.6 | async-start | bytes 524288 | tf_op jit(solution)/shard_map/all_to_all | solution.py:143
  160.1 1.2 copy-start.2
  166.7 30.4 %all-to-all-start.7 = ((bf16[16,20,512]{2,1,0:T(8,128)(2,1)}), bf16[16,20,512]{2,1,0:T(8,128)(2,1)S(1)}, u32[]{:S(2)}, u32[]{:S(2)}) async-start(bf16[16,20,512]{2,1,0:T(8,128)(2,1)} %reshape.183), calls=%async_computation.7 | async-start | bytes 786432 | tf_op jit(solution)/shard_map/all_to_all | solution.py:18
  200.0 29.9 %all-to-all-start.8 = ((bf16[16,20,512]{2,1,0:T(8,128)(2,1)}), bf16[16,20,512]{2,1,0:T(8,128)(2,1)S(1)}, u32[]{:S(2)}, u32[]{:S(2)}) async-start(bf16[16,20,512]{2,1,0:T(8,128)(2,1)} %broadcast_in_dim.31), calls=%async_computation.8 | async-start | bytes 786432 | tf_op jit(solution)/shard_map/all_to_all | solution.py:30

commit v2 on v1

v2 whole, which is shorter than its diff:
```python
import functools

import jax
import jax.numpy as jnp
from jax import lax
from jax.experimental import pallas as pl
from jax.experimental.pallas import tpu as pltpu
from jax.sharding import PartitionSpec as P

F32 = jnp.float32
BF16 = jnp.bfloat16
I32 = jnp.int32
MESH = pl.DeviceIdType.MESH
CAP = 8


def mark(condition):
    return jnp.where(condition, 1.0, 0.0).astype(BF16)


def iota(shape, dim):
    return lax.broadcasted_iota(I32, shape, dim)


def mm(a, b):
    return jnp.dot(a, b, preferred_element_type=F32)


def mm_rows(a, b):
    return lax.dot_general(a, b, (((1,), (1,)), ((), ())), preferred_element_type=F32)


def mm_cols(a, b):
    return lax.dot_general(a, b, (((0,), (0,)), ((), ())), preferred_element_type=F32)


def norm_rows(v):
    centred = v - jnp.mean(v, axis=-1, keepdims=True)
    spread = jnp.mean(centred * centred, axis=-1, keepdims=True)
    return centred * lax.rsqrt(spread + 1e-05)


def silu(v):
    return v * jax.nn.sigmoid(v)


def tail(preact, weight):
    return norm_rows(mm(silu(preact).astype(BF16), weight))


def kernel(
    nb, np_, ny,
    gf_h, gi_h, go_h, gw, ee_h, en_h, pe_h, pn_h, mn_h, me_h,
    tgt, snd, nod, geo, msd, mrc, halo,
    two_ref, edge_ref,
    gf, gi, go, ee, en, pe, pn, mn, me, wsem,
    addr_out, addr_in, outbox, inbox, rs_out, rs_in, ag_out, ag_in,
    halo_out, halo_in, rs2_out, rs2_in, ag2_out, ag2_in,
    recv_proj, edge_proj, one_ref, ssem, rsem,
):
    b = lax.axis_index("band")
    p = lax.axis_index("patch")
    edges = tgt.shape[1]
    count, width = mn.shape
    half = width // 2
    share = count // nb
    block = 2 * share
    slots = np_ * CAP
    grid_rows = gf.shape[0]
    medges = me.shape[0]
    padded = -(-share // 16) * 16
    wide = 2 * count

    def peer(i):
        off = (i * 29) % np_
        x = (p // (2 * ny) + off // (2 * ny)) % (np_ // (2 * ny))
        y = (p // 2 + off // 2) % ny
        c = (p + off) % 2
        return x * (2 * ny) + y * 2 + c

    def level(i):
        return (b + i * 7) % nb

    barrier = pltpu.get_barrier_semaphore()

    def greet_patch(i, carry):
        pl.semaphore_signal(barrier, inc=1, device_id={"patch": peer(i)}, device_id_type=MESH)
        return carry

    def greet_band(i, carry):
        pl.semaphore_signal(barrier, inc=1, device_id={"band": level(i)}, device_id_type=MESH)
        return carry

    lax.fori_loop(1, np_, greet_patch, 0)
    lax.fori_loop(1, nb, greet_band, 0)

    loads = [
        pltpu.make_async_copy(src, dst, wsem.at[k])
        for k, (src, dst) in enumerate(
            [(gf_h, gf), (gi_h, gi), (go_h, go), (ee_h, ee), (mn_h, mn), (me_h, me),
             (pe_h, pe), (en_h, en), (pn_h, pn)]
        )
    ]
    for load in loads:
        load.start()

    def to_patches(src, dst, k):
        def step(i, carry):
            q = peer(i)
            pltpu.make_async_remote_copy(
                src_ref=src.at[q], dst_ref=dst.at[p], send_sem=ssem.at[k], recv_sem=rsem.at[k],
                device_id={"patch": q}, device_id_type=MESH,
            ).start()
            return carry

        lax.fori_loop(1, np_, step, 0)
        dst[p] = src[p]

    def to_bands(src, dst, k, same):
        def step(i, carry):
            q = level(i)
            pltpu.make_async_remote_copy(
                src_ref=src if same else src.at[q], dst_ref=dst.at[b],
                send_sem=ssem.at[k], recv_sem=rsem.at[k],
                device_id={"band": q}, device_id_type=MESH,
            ).start()
            return carry

        lax.fori_loop(1, nb, step, 0)
        dst[b] = src[...] if same else src[b]

    def settle(dst, sems, k):
        view = dst.at[pl.ds(0, dst.shape[0] - 1)]
        pltpu.make_async_copy(view, view, sems.at[k]).wait()

    target = tgt[...]
    named = mark(iota((np_, edges), 0) == target)
    before = mark(iota((edges, edges), 0) < iota((edges, edges), 1))
    rank = mm(named, before)
    slot = jnp.sum(rank * named.astype(F32), axis=0, keepdims=True).astype(I32)
    chosen = mark(iota((slots, edges), 0) == target * CAP + slot)
    lanes = iota((128, edges), 0)
    mine = (lanes % CAP == slot) & (lanes // CAP == p % 16)
    node = nod[...] + 1
    high = jnp.where(mine, (node >> 6).astype(F32), 0.0).astype(BF16)
    low = jnp.where(mine, (node & 63).astype(F32), 0.0).astype(BF16)
    addr_out[:, 0, :] = 64.0 * mm_rows(named, high) + mm_rows(named, low)
    from_grid = mm_rows(chosen, mark(iota((grid_rows, edges), 0) == snd[...])).astype(BF16)
    geo_rows = mm_rows(chosen, geo[...]).astype(BF16)

    loads[0].wait()
    loads[1].wait()
    hidden = silu(mm(gf[...], gi[...])).astype(BF16)
    loads[2].wait()
    latent = norm_rows(mm(hidden, go[...])).astype(BF16)
    loads[3].wait()
    sender_proj = mm(latent, ee[0]).astype(BF16)
    terms = mm(from_grid, sender_proj) + mm(geo_rows, gw[...])
    outbox[...] = terms.reshape(np_, CAP, width).astype(BF16)

    pl.semaphore_wait(barrier, np_ + nb - 2)
    to_patches(addr_out, addr_in, 0)
    to_patches(outbox, inbox, 1)

    loads[4].wait()
    recv_proj[...] = mm(mn[...], ee[1]).astype(BF16)
    loads[5].wait()
    loads[6].wait()
    edge_proj[...] = mm(me[...], pe[0])
    loads[7].wait()
    loads[8].wait()
    row = iota((padded, count), 0)
    own_pick = mark((iota((padded, count), 1) == b * share + row) & (row < share))
    own = mm(own_pick, mn[...]).astype(BF16)
    own_proj = mm(own, en[0])
    row, col = iota((padded, block), 0), iota((padded, block), 1)
    to_left = mark((row == col) & (row < share))
    to_right = mark(col == row + share)
    row, col = iota((block, padded), 0), iota((block, padded), 1)
    from_left = mark((row == col) & (row < share))
    from_right = mark(row == col + share)
    where_row = iota((wide, 1), 0).astype(F32)
    where_band = jnp.floor((where_row + 0.5) * (1.0 / block))
    within = where_row - block * where_band
    wide_node = where_band * share + jnp.where(within < share, within, within - share)
    left_rows = jnp.broadcast_to(within, (wide, half)) < share

    def in_halves(rows):
        picked = jnp.where(left_rows, rows[:, :half], rows[:, half:])
        return picked.reshape(nb, block, half).astype(BF16)

    def update(rows, rows_proj, arrived, weights):
        agg = jnp.sum(arrived[...].astype(F32), axis=0).astype(BF16)
        agg_left = mm(to_left, agg).astype(BF16)
        agg_right = mm(to_right, agg).astype(BF16)
        preact = rows_proj + mm(agg_left, weights[1, :half]) + mm(agg_right, weights[1, half:])
        return (rows.astype(F32) + tail(preact, weights[2])).astype(BF16)

    def packed(rows):
        return (mm(from_left, rows[:, :half]) + mm(from_right, rows[:, half:])).astype(BF16)

    def natural(arrived, out):
        flat = arrived[...].astype(F32).reshape(wide, half).astype(BF16)
        row = iota((count, wide), 0).astype(F32)
        place = row + share * jnp.floor((row + 0.5) * (1.0 / share))
        col = iota((count, wide), 1).astype(F32)
        out[:, :half] = mm(mark(col == place), flat).astype(BF16)
        out[:, half:] = mm(mark(col == place + share), flat).astype(BF16)

    settle(addr_in, rsem, 0)
    per = min(16, np_)
    placed = jnp.sum(addr_in[:, 0, :].reshape(np_ // per, per, 128), axis=1)
    span = per * CAP
    pieces = [placed[k : k + 1, :span] for k in range(np_ // per)]
    node_rows = iota((count, span), 0).astype(F32) + 1.0
    landing = jnp.concatenate([mark(node_rows == v) for v in pieces], axis=1)
    wide_landing = jnp.concatenate(
        [mark(jnp.broadcast_to(wide_node + 1.0, (wide, span)) == v) for v in pieces], axis=1
    )
    gathered = mm_cols(landing, recv_proj[...])

    settle(inbox, rsem, 1)
    preact = inbox[...].astype(F32).reshape(slots, width) + gathered
    message = tail(preact, ee[2]).astype(BF16)
    rs_out[...] = in_halves(mm(wide_landing, message))
    to_bands(rs_out, rs_in, 2, False)
    settle(rs_in, rsem, 2)
    first = update(own, own_proj, rs_in, en)
    ag_out[...] = packed(first)
    to_bands(ag_out, ag_in, 3, True)
    first_proj = mm(first, pn[0])

    spread_to = iota((np_ * 4, slots), 1)
    spread_from = iota((np_ * 4, slots), 0)
    spread = mark(spread_from == (spread_to >> 3) * 4 + (spread_to & 3))
    rows = jnp.broadcast_to(halo[...], (8, np_ * 4))
    wanted = 64.0 * mm((rows >> 6).astype(F32).astype(BF16), spread) + mm(
        (rows & 63).astype(F32).astype(BF16), spread
    )
    halo_pick = mark(iota((count, slots), 0).astype(F32) == wanted[0:1, :])
    left_slots = (iota((slots, half), 0) & 7) < 4
    local_pick = mark(iota((count, medges), 0) == msd[...])
    recv_pick = mark(iota((count, medges), 0) == mrc[...])
    ghost = msd[...] - count
    ghost_row = jnp.where(ghost < 0, -1024, (ghost >> 2) * 8 + (ghost & 3))
    ghost_left = mark(iota((slots, medges), 0) == ghost_row)
    ghost_right = mark(iota((slots, medges), 0) == ghost_row + 4)
    wide_recv = mark(
        jnp.broadcast_to(wide_node, (wide, medges)) == mrc[...].astype(F32)
    )

    settle(ag_in, rsem, 3)
    natural(ag_in, one_ref)
    sent = mm(one_ref[...], pe[1]).astype(BF16)
    going = mm_cols(halo_pick, sent)
    going = jnp.where(left_slots, going[:, :half], going[:, half:])
    halo_out[...] = going.reshape(np_, CAP, half).astype(BF16)
    to_patches(halo_out, halo_in, 4)
    recv_two = mm(one_ref[...], pe[2]).astype(BF16)
    edge_proj[...] += mm_cols(local_pick, sent) + mm_cols(recv_pick, recv_two)

    settle(halo_in, rsem, 4)
    ghosts = halo_in[...].astype(F32).reshape(slots, half).astype(BF16)
    edge_proj[:, :half] += mm_cols(ghost_left, ghosts)
    edge_proj[:, half:] += mm_cols(ghost_right, ghosts)
    edge_new = (me[...].astype(F32) + tail(edge_proj[...], pe[3])).astype(BF16)
    rs2_out[...] = in_halves(mm(wide_recv, edge_new))
    to_bands(rs2_out, rs2_in, 5, False)
    edge_ref[...] = edge_new
    settle(rs2_in, rsem, 5)
    second = update(first, first_proj, rs2_in, pn)
    ag2_out[...] = packed(second)
    to_bands(ag2_out, ag2_in, 6, True)
    settle(ag2_in, rsem, 6)
    natural(ag2_in, two_ref)

    settle(addr_in, ssem, 0)
    settle(inbox, ssem, 1)
    settle(rs_in, ssem, 2)
    settle(ag_in, ssem, 3)
    settle(halo_in, ssem, 4)
    settle(rs2_in, ssem, 5)
    settle(ag2_in, ssem, 6)


def per_device(
    nb, np_, ny,
    grid_feat, enc_sender, enc_patch, enc_node, enc_geo, mesh_nodes, mesh_edge, mesh_send,
    mesh_recv, halo_rows, grid_in, grid_out, geo_weight, enc_edge_w, enc_node_w, proc_edge_w,
    proc_node_w,
):
    edges = enc_sender.shape[0]
    count, width = mesh_nodes.shape
    medges = mesh_edge.shape[0]
    half = width // 2
    block = 2 * count // nb
    slots = np_ * CAP
    whole = pl.BlockSpec(memory_space=pltpu.VMEM)
    away = pl.BlockSpec(memory_space=pl.ANY)

    def like(v):
        return pltpu.VMEM(v.shape, v.dtype)

    return pl.pallas_call(
        functools.partial(kernel, nb, np_, ny),
        out_shape=(
            jax.ShapeDtypeStruct((count, width), BF16),
            jax.ShapeDtypeStruct((medges, width), BF16),
        ),
        in_specs=[away] * 3 + [whole] + [away] * 6 + [whole] * 7,
        out_specs=(whole, whole),
        scratch_shapes=[
            like(grid_feat), like(grid_in), like(grid_out), like(enc_edge_w), like(enc_node_w),
            like(proc_edge_w), like(proc_node_w), like(mesh_nodes), like(mesh_edge),
            pltpu.SemaphoreType.DMA((9,)),
            pltpu.VMEM((np_, 1, 128), F32), pltpu.VMEM((np_, 1, 128), F32),
            pltpu.VMEM((np_, CAP, width), BF16), pltpu.VMEM((np_, CAP, width), BF16),
            pltpu.VMEM((nb, block, half), BF16), pltpu.VMEM((nb, block, half), BF16),
            pltpu.VMEM((block, half), BF16), pltpu.VMEM((nb, block, half), BF16),
            pltpu.VMEM((np_, CAP, half), BF16), pltpu.VMEM((np_, CAP, half), BF16),
            pltpu.VMEM((nb, block, half), BF16), pltpu.VMEM((nb, block, half), BF16),
            pltpu.VMEM((block, half), BF16), pltpu.VMEM((nb, block, half), BF16),
            pltpu.VMEM((count, width), BF16), pltpu.VMEM((medges, width), F32),
            pltpu.VMEM((count, width), BF16),
            pltpu.SemaphoreType.DMA((7,)), pltpu.SemaphoreType.DMA((7,)),
        ],
        compiler_params=pltpu.CompilerParams(collective_id=0, has_side_effects=True),
    )(
        grid_feat, grid_in, grid_out, geo_weight, enc_edge_w, enc_node_w, proc_edge_w,
        proc_node_w, mesh_nodes, mesh_edge,
        enc_patch.reshape(1, edges), enc_sender.reshape(1, edges), enc_node.reshape(1, edges),
        enc_geo, mesh_send.reshape(1, medges), mesh_recv.reshape(1, medges), halo_rows,
    )


def solution(mesh):
    both = ("band", "patch")
    nb, np_ = mesh.shape["band"], mesh.shape["patch"]
    ny = 8 if np_ == 64 else np_ // 4
    placed = (
        P(both, None), P(both), P(both, None), P(both), P(None, both), P("patch", None),
        P(both, None), P(both), P(both), P("patch", None),
    ) + (P(),) * 7
    return jax.shard_map(
        functools.partial(per_device, nb, np_, ny),
        mesh=mesh,
        in_specs=placed,
        out_specs=(P("patch", None), P(both, None)),
        check_vma=False,
    )
```

time: 232 us -> 138 us (0.59)
  Pallas kernels: 0 us -> 128 us
  waiting for transfers between devices: 113 us -> 0 us
  starting transfers between devices: 73.8 us -> 0 us
  matrix products: 16.3 us -> 0 us
  other arithmetic: 9.95 us -> 0 us
  local copies, waits for them, and re-layouts: 16.3 us -> 7.68 us
    pallas_call x0 -> x1, Pallas kernels: none -> 128 us  [per_device(): pl.pallas_call(functools.partial(kernel, nb, np_, ny), out_shape=(jax.Sha...]
    all_to_all x9 -> x0, waiting for transfers between devices: 113 us -> none  [the longest x2 43.6 us: from_everyone(): lax.all_to_all(jnp.broadcast_to(value[None], (length, *value.shape)), axi...]
    all_to_all x9 -> x0, starting transfers between devices: 73.8 us -> none  [the longest x4 29.3 us: exchange_in_order(): lax.all_to_all(pieces, axes[k], split_axis=k, concat_axis=k, tiled=True)]
    dot_general x13 -> x0, matrix products: 16.3 us -> none  [the longest x4 5.54 us: network_tail(): jnp.dot(hidden, out_weight, preferred_element_type=jnp.float32)]
    gather x5 -> x0, local copies, waits for them, and re-layouts: 7.14 us -> none  [the longest x1 2.24 us: per_device(): send_term = (sender_proj[enc_sender] + geo_term).astype(jnp.bfloat16)]
    unnamed x20 -> x3, local copies, waits for them, and re-layouts: 0.8 us -> 5.17 us
    scatter-add x1 -> x0, other arithmetic: 2.39 us -> none  [per_device(): jnp.zeros((mesh_count, latent_width), jnp.float32).at[mesh_recv]]
  transfers between devices with their start and end apart: 9 -> 0, of which waited for: 7 -> 0; matrix products, arithmetic and copies ran while one was open for 8% -> 0% of each run, Pallas kernels for 0% -> 0%
where the time goes in v2:
time: 138 us; the launch traced here: 137 us
  Pallas kernels  128 us (93%)
  local copies, waits for them, and re-layouts  7.68 us (6%)
    pallas_call x1, Pallas kernels, per_device(): pl.pallas_call(functools.partial(kernel, nb, np_, ny), out_shape=(jax.Sha...  128 us
    unnamed x3, local copies, waits for them, and re-layouts  5.17 us

profile of v2, /device:TPU:6, one launch (start us, length us, event | category | flops | bytes accessed | tf_op | source)
XLA Modules:
  0.0 136.8 jit_solution(13378518141409632146)
XLA Ops:
  0.6 1.2 reshape.20.snd
  1.9 1.3 reshape.21.nod
  3.1 1.8 %copy.19.gf_h = bf16[256,474]{1,0:T(8,128)(2,1)} copy(bf16[256,474]{0,1:T(8,128)(2,1)} %param.17) | data formatting | bytes 485376 | tf_op args[0]
  4.9 128.5 %shard_map.176 = (bf16[320,512]{1,0:T(8,128)(2,1)}, bf16[256,512]{1,0:T(8,128)(2,1)}) custom-call(bf16[256,474]{1,0:T(8,128)(2,1)} %copy.19.gf_h, bf16[474,512]{1,0:T(8,128)(2,1)} %gi_h.1, bf16[512,512]{1,0:T(8,128)(2,1)} %go_h.1, bf16[4,512]{1,0:T(4,128)(2,1)} %gw.1, bf16[3,512,512]{2,1,0:T(8,128)(2,1)} %ee_h.1, bf16[3,512,512]{2,1,0:T(8,128)(2,1)} %en_h.1, ...), custom_call_target="tpu_custom_call" | custom-call | tf_op jit(solution)/shard_map/pallas_call | solution.py:304
  133.4 1.7 %copy.22 = bf16[320,512]{1,0:T(8,128)(2,1)} copy(bf16[320,512]{1,0:T(8,128)(2,1)} %get-tuple-element.4) | data formatting | bytes 655360
  135.1 1.7 %copy.23 = bf16[256,512]{1,0:T(8,128)(2,1)} copy(bf16[256,512]{1,0:T(8,128)(2,1)} %get-tuple-element.5) | data formatting | bytes 524288

commit v3 on v2

--- a/solution.py
+++ b/solution.py
@@ -56,7 +56,8 @@
     gf, gi, go, ee, en, pe, pn, mn, me, wsem,
     addr_out, addr_in, outbox, inbox, rs_out, rs_in, ag_out, ag_in,
     halo_out, halo_in, rs2_out, rs2_in, ag2_out, ag2_in,
-    recv_proj, edge_proj, one_ref, ssem, rsem,
+    via_in, via_out, via2_in, via2_out, left_pick, right_pick,
+    recv_proj, edge_proj, one_ref, placed, total, ssem, rsem,
 ):
     b = lax.axis_index("band")
     p = lax.axis_index("patch")
@@ -66,33 +67,32 @@
     share = count // nb
     block = 2 * share
     slots = np_ * CAP
-    grid_rows = gf.shape[0]
+    grid_rows = gf.shape[1]
     medges = me.shape[0]
     padded = -(-share // 16) * 16
+    cut = -(-share // 8) * 8
     wide = 2 * count
 
-    def peer(i):
-        off = (i * 29) % np_
-        x = (p // (2 * ny) + off // (2 * ny)) % (np_ // (2 * ny))
-        y = (p // 2 + off // 2) % ny
-        c = (p + off) % 2
-        return x * (2 * ny) + y * 2 + c
-
-    def level(i):
-        return (b + i * 7) % nb
-
-    barrier = pltpu.get_barrier_semaphore()
-
-    def greet_patch(i, carry):
-        pl.semaphore_signal(barrier, inc=1, device_id={"patch": peer(i)}, device_id_type=MESH)
-        return carry
-
-    def greet_band(i, carry):
-        pl.semaphore_signal(barrier, inc=1, device_id={"band": level(i)}, device_id_type=MESH)
-        return carry
-
-    lax.fori_loop(1, np_, greet_patch, 0)
-    lax.fori_loop(1, nb, greet_band, 0)
+    per = 2 * ny
+    nx = np_ // per
+    x0, y0, c0 = p // per, (p // 2) % ny, p % 2
+    steps = [(ny // 2 + (k + 1) // 2 * (1 if k % 2 else -1)) % ny for k in range(ny)]
+    spots = [
+        ((dy, c), (y0 + dy) % ny * 2 + (c0 + c) % 2) for dy in steps for c in range(2)
+    ]
+
+    def each_peer(visit):
+        for where, spot in spots:
+            if where != (0, 0):
+                visit(x0 * per + spot, 0)
+
+        def column(dx, carry):
+            first = (x0 + dx) % nx * per
+            for _, spot in spots:
+                visit(first + spot, dx)
+            return carry
+
+        lax.fori_loop(1, nx, column, 0)
 
     loads = [
         pltpu.make_async_copy(src, dst, wsem.at[k])
@@ -104,30 +104,80 @@
     for load in loads:
         load.start()
 
-    def to_patches(src, dst, k):
-        def step(i, carry):
-            q = peer(i)
+    barrier = pltpu.get_barrier_semaphore()
+
+    def greet(axis, q):
+        pl.semaphore_signal(barrier, inc=1, device_id={axis: q}, device_id_type=MESH)
+
+    each_peer(lambda q, dx: greet("patch", q))
+    for k in range(1, nb):
+        greet("band", (b + k) % nb)
+
+    def to_patches(src, dst, send, recv, apart):
+        def visit(q, dx):
             pltpu.make_async_remote_copy(
-                src_ref=src.at[q], dst_ref=dst.at[p], send_sem=ssem.at[k], recv_sem=rsem.at[k],
+                src_ref=src.at[q], dst_ref=dst.at[p], send_sem=ssem.at[send],
+                recv_sem=rsem.at[recv + dx if apart else recv],
                 device_id={"patch": q}, device_id_type=MESH,
             ).start()
-            return carry
-
-        lax.fori_loop(1, np_, step, 0)
+
+        each_peer(visit)
         dst[p] = src[p]
 
-    def to_bands(src, dst, k, same):
-        def step(i, carry):
-            q = level(i)
-            pltpu.make_async_remote_copy(
-                src_ref=src if same else src.at[q], dst_ref=dst.at[b],
-                send_sem=ssem.at[k], recv_sem=rsem.at[k],
-                device_id={"band": q}, device_id_type=MESH,
-            ).start()
-            return carry
-
-        lax.fori_loop(1, nb, step, 0)
-        dst[b] = src[...] if same else src[b]
+    sides = ((0, 1, pl.ds(0, cut)), (1, -1, pl.ds(cut, block - cut)))
+
+    def to_band(src, dst, send, recv, q):
+        pltpu.make_async_remote_copy(
+            src_ref=src, dst_ref=dst, send_sem=ssem.at[send], recv_sem=rsem.at[recv],
+            device_id={"band": q}, device_id_type=MESH,
+        ).start()
+
+    def wait_for(view, sem):
+        pltpu.make_async_copy(view, view, sem).wait()
+
+    def reduce_bands(src, via, sums, dst, send, recv, last):
+        for k in (4, 3, 2, 1):
+            for side, sign, rows in sides:
+                q = (b + nb - sign * k) % nb
+                o = (b + nb - sign * (k + 4)) % nb
+                if k == 4:
+                    to_band(src.at[o, rows], via.at[6, rows], send, last + side, q)
+                else:
+                    to_band(src.at[o], via.at[side * 3 + k - 1], send, recv + side, q)
+        for k in (3, 2, 1):
+            for side, sign, rows in sides:
+                q = (b + nb - sign * k) % nb
+                to_band(src.at[q], dst.at[side * 3 + k - 1], send, recv + 2, q)
+        for side, sign, rows in sides:
+            q = (b + nb - sign * 4) % nb
+            wait_for(via.at[pl.ds(0, 3)], rsem.at[recv + side])
+            wait_for(via.at[6, rows], rsem.at[last + side])
+            value = src[q].astype(F32)
+            for k in range(3):
+                value = value + via[side * 3 + k].astype(F32)
+            sums[side] = value.astype(BF16)
+            part = slice(rows.start, rows.start + rows.size)
+            sums[side, part] = (value[part] + via[6, part].astype(F32)).astype(BF16)
+            to_band(sums.at[side], dst.at[6 + side], send, recv + 2, q)
+
+    def reduced(src, dst, recv):
+        wait_for(dst.at[pl.ds(0, 8)], rsem.at[recv + 2])
+        return src[b].astype(F32) + jnp.sum(dst[...].astype(F32), axis=0)
+
+    def gather_bands(src, dst, send, recv):
+        for k in (4, 3, 2, 1):
+            for side, sign, rows in sides:
+                sem = recv + side if k == 4 else recv + 2
+                to_band(src, dst.at[b], send, sem, (b + nb + sign * k) % nb)
+        dst[b] = src[...]
+
+    def relay_bands(dst, send, recv):
+        for side, sign, rows in sides:
+            o = (b + nb - sign * 4) % nb
+            wait_for(dst.at[0], rsem.at[recv + side])
+            to_band(dst.at[o, rows], dst.at[o, rows], send, recv + 2, (b + nb + sign * 4) % nb)
+            for k in (3, 2, 1):
+                to_band(dst.at[o], dst.at[o], send, recv + 2, (b + nb + sign * k) % nb)
 
     def settle(dst, sems, k):
         view = dst.at[pl.ds(0, dst.shape[0] - 1)]
@@ -140,17 +190,17 @@
     slot = jnp.sum(rank * named.astype(F32), axis=0, keepdims=True).astype(I32)
     chosen = mark(iota((slots, edges), 0) == target * CAP + slot)
     lanes = iota((128, edges), 0)
-    mine = (lanes % CAP == slot) & (lanes // CAP == p % 16)
-    node = nod[...] + 1
+    mine = (lanes % CAP == slot) & (lanes // CAP == p % per)
+    node = nod[...].reshape(1, edges) + 1
     high = jnp.where(mine, (node >> 6).astype(F32), 0.0).astype(BF16)
     low = jnp.where(mine, (node & 63).astype(F32), 0.0).astype(BF16)
     addr_out[:, 0, :] = 64.0 * mm_rows(named, high) + mm_rows(named, low)
-    from_grid = mm_rows(chosen, mark(iota((grid_rows, edges), 0) == snd[...])).astype(BF16)
+    from_grid = mm_rows(chosen, mark(iota((grid_rows, edges), 0) == snd[...].reshape(1, edges))).astype(BF16)
     geo_rows = mm_rows(chosen, geo[...]).astype(BF16)
 
     loads[0].wait()
     loads[1].wait()
-    hidden = silu(mm(gf[...], gi[...])).astype(BF16)
+    hidden = silu(mm_cols(gf[...], gi[...])).astype(BF16)
     loads[2].wait()
     latent = norm_rows(mm(hidden, go[...])).astype(BF16)
     loads[3].wait()
@@ -159,8 +209,8 @@
     outbox[...] = terms.reshape(np_, CAP, width).astype(BF16)
 
     pl.semaphore_wait(barrier, np_ + nb - 2)
-    to_patches(addr_out, addr_in, 0)
-    to_patches(outbox, inbox, 1)
+    to_patches(addr_out, addr_in, 0, 0, False)
+    to_patches(outbox, inbox, 1, 19, True)
 
     loads[4].wait()
     recv_proj[...] = mm(mn[...], ee[1]).astype(BF16)
@@ -190,7 +240,7 @@
         return picked.reshape(nb, block, half).astype(BF16)
 
     def update(rows, rows_proj, arrived, weights):
-        agg = jnp.sum(arrived[...].astype(F32), axis=0).astype(BF16)
+        agg = arrived.astype(BF16)
         agg_left = mm(to_left, agg).astype(BF16)
         agg_right = mm(to_right, agg).astype(BF16)
         preact = rows_proj + mm(agg_left, weights[1, :half]) + mm(agg_right, weights[1, half:])
@@ -199,35 +249,42 @@
     def packed(rows):
         return (mm(from_left, rows[:, :half]) + mm(from_right, rows[:, half:])).astype(BF16)
 
+    row = iota((count, wide), 0).astype(F32)
+    place = row + share * jnp.floor((row + 0.5) * (1.0 / share))
+    col = iota((count, wide), 1).astype(F32)
+    left_pick[...] = mark(col == place)
+    right_pick[...] = mark(col == place + share)
+
     def natural(arrived, out):
         flat = arrived[...].astype(F32).reshape(wide, half).astype(BF16)
-        row = iota((count, wide), 0).astype(F32)
-        place = row + share * jnp.floor((row + 0.5) * (1.0 / share))
-        col = iota((count, wide), 1).astype(F32)
-        out[:, :half] = mm(mark(col == place), flat).astype(BF16)
-        out[:, half:] = mm(mark(col == place + share), flat).astype(BF16)
+        out[:, :half] = mm(left_pick[...], flat).astype(BF16)
+        out[:, half:] = mm(right_pick[...], flat).astype(BF16)
 
     settle(addr_in, rsem, 0)
-    per = min(16, np_)
-    placed = jnp.sum(addr_in[:, 0, :].reshape(np_ // per, per, 128), axis=1)
     span = per * CAP
-    pieces = [placed[k : k + 1, :span] for k in range(np_ // per)]
+    placed[:, 0, :] = jnp.sum(addr_in[:, 0, :].reshape(nx, per, 128), axis=1)
     node_rows = iota((count, span), 0).astype(F32) + 1.0
-    landing = jnp.concatenate([mark(node_rows == v) for v in pieces], axis=1)
-    wide_landing = jnp.concatenate(
-        [mark(jnp.broadcast_to(wide_node + 1.0, (wide, span)) == v) for v in pieces], axis=1
-    )
-    gathered = mm_cols(landing, recv_proj[...])
-
-    settle(inbox, rsem, 1)
-    preact = inbox[...].astype(F32).reshape(slots, width) + gathered
-    message = tail(preact, ee[2]).astype(BF16)
-    rs_out[...] = in_halves(mm(wide_landing, message))
-    to_bands(rs_out, rs_in, 2, False)
-    settle(rs_in, rsem, 2)
-    first = update(own, own_proj, rs_in, en)
+    wide_rows = jnp.broadcast_to(wide_node + 1.0, (wide, span))
+    for dx in range(nx):
+        x = (x0 + nx - dx) % nx
+        names = placed[x][:, :span]
+        gathered = mm_cols(mark(node_rows == names), recv_proj[...])
+        wide_landing = mark(wide_rows == names)
+        wait_for(inbox.at[pl.ds(0, per - 1 if dx == 0 else per)], rsem.at[19 + dx])
+        arrived = inbox[pl.ds(x * per, per)].astype(F32).reshape(span, width)
+        message = tail(arrived + gathered, ee[2]).astype(BF16)
+        landed = mm(wide_landing, message)
+        if dx == 0:
+            total[...] = landed
+        elif dx < nx - 1:
+            total[...] += landed
+        else:
+            rs_out[...] = in_halves(total[...] + landed)
+    reduce_bands(rs_out, via_in, via_out, rs_in, 2, 7, 19 + nx)
+    first = update(own, own_proj, reduced(rs_out, rs_in, 7), en)
     ag_out[...] = packed(first)
-    to_bands(ag_out, ag_in, 3, True)
+    gather_bands(ag_out, ag_in, 3, 10)
+    relay_bands(ag_in, 3, 10)
     first_proj = mm(first, pn[0])
 
     spread_to = iota((np_ * 4, slots), 1)
@@ -249,13 +306,13 @@
         jnp.broadcast_to(wide_node, (wide, medges)) == mrc[...].astype(F32)
     )
 
-    settle(ag_in, rsem, 3)
+    wait_for(ag_in.at[pl.ds(0, 13)], rsem.at[12])
     natural(ag_in, one_ref)
     sent = mm(one_ref[...], pe[1]).astype(BF16)
     going = mm_cols(halo_pick, sent)
     going = jnp.where(left_slots, going[:, :half], going[:, half:])
     halo_out[...] = going.reshape(np_, CAP, half).astype(BF16)
-    to_patches(halo_out, halo_in, 4)
+    to_patches(halo_out, halo_in, 4, 4, False)
     recv_two = mm(one_ref[...], pe[2]).astype(BF16)
     edge_proj[...] += mm_cols(local_pick, sent) + mm_cols(recv_pick, recv_two)
 
@@ -265,21 +322,21 @@
     edge_proj[:, half:] += mm_cols(ghost_right, ghosts)
     edge_new = (me[...].astype(F32) + tail(edge_proj[...], pe[3])).astype(BF16)
     rs2_out[...] = in_halves(mm(wide_recv, edge_new))
-    to_bands(rs2_out, rs2_in, 5, False)
+    reduce_bands(rs2_out, via2_in, via2_out, rs2_in, 5, 13, 21 + nx)
     edge_ref[...] = edge_new
-    settle(rs2_in, rsem, 5)
-    second = update(first, first_proj, rs2_in, pn)
+    second = update(first, first_proj, reduced(rs2_out, rs2_in, 13), pn)
     ag2_out[...] = packed(second)
-    to_bands(ag2_out, ag2_in, 6, True)
-    settle(ag2_in, rsem, 6)
+    gather_bands(ag2_out, ag2_in, 6, 16)
+    relay_bands(ag2_in, 6, 16)
+    wait_for(ag2_in.at[pl.ds(0, 13)], rsem.at[18])
     natural(ag2_in, two_ref)
 
     settle(addr_in, ssem, 0)
     settle(inbox, ssem, 1)
-    settle(rs_in, ssem, 2)
+    settle(rs_out, ssem, 2)
     settle(ag_in, ssem, 3)
     settle(halo_in, ssem, 4)
-    settle(rs2_in, ssem, 5)
+    settle(rs2_out, ssem, 5)
     settle(ag2_in, ssem, 6)
 
 
@@ -304,31 +361,35 @@
     return pl.pallas_call(
         functools.partial(kernel, nb, np_, ny),
         out_shape=(
-            jax.ShapeDtypeStruct((count, width), BF16),
-            jax.ShapeDtypeStruct((medges, width), BF16),
+            pltpu.VMEM((count, width), BF16),
+            pltpu.VMEM((medges, width), BF16),
         ),
         in_specs=[away] * 3 + [whole] + [away] * 6 + [whole] * 7,
         out_specs=(whole, whole),
         scratch_shapes=[
-            like(grid_feat), like(grid_in), like(grid_out), like(enc_edge_w), like(enc_node_w),
+            pltpu.VMEM(grid_feat.shape[::-1], BF16), like(grid_in), like(grid_out), like(enc_edge_w), like(enc_node_w),
             like(proc_edge_w), like(proc_node_w), like(mesh_nodes), like(mesh_edge),
             pltpu.SemaphoreType.DMA((9,)),
             pltpu.VMEM((np_, 1, 128), F32), pltpu.VMEM((np_, 1, 128), F32),
             pltpu.VMEM((np_, CAP, width), BF16), pltpu.VMEM((np_, CAP, width), BF16),
-            pltpu.VMEM((nb, block, half), BF16), pltpu.VMEM((nb, block, half), BF16),
+            pltpu.VMEM((nb, block, half), BF16), pltpu.VMEM((8, block, half), BF16),
             pltpu.VMEM((block, half), BF16), pltpu.VMEM((nb, block, half), BF16),
             pltpu.VMEM((np_, CAP, half), BF16), pltpu.VMEM((np_, CAP, half), BF16),
-            pltpu.VMEM((nb, block, half), BF16), pltpu.VMEM((nb, block, half), BF16),
+            pltpu.VMEM((nb, block, half), BF16), pltpu.VMEM((8, block, half), BF16),
             pltpu.VMEM((block, half), BF16), pltpu.VMEM((nb, block, half), BF16),
+            pltpu.VMEM((7, block, half), BF16), pltpu.VMEM((2, block, half), BF16),
+            pltpu.VMEM((7, block, half), BF16), pltpu.VMEM((2, block, half), BF16),
+            pltpu.VMEM((count, 2 * count), BF16), pltpu.VMEM((count, 2 * count), BF16),
             pltpu.VMEM((count, width), BF16), pltpu.VMEM((medges, width), F32),
             pltpu.VMEM((count, width), BF16),
-            pltpu.SemaphoreType.DMA((7,)), pltpu.SemaphoreType.DMA((7,)),
+            pltpu.VMEM((np_ // (2 * ny), 1, 128), F32), pltpu.VMEM((2 * count, width), F32),
+            pltpu.SemaphoreType.DMA((7,)), pltpu.SemaphoreType.DMA((23 + np_ // (2 * ny),)),
         ],
         compiler_params=pltpu.CompilerParams(collective_id=0, has_side_effects=True),
     )(
-        grid_feat, grid_in, grid_out, geo_weight, enc_edge_w, enc_node_w, proc_edge_w,
+        grid_feat.T, grid_in, grid_out, geo_weight, enc_edge_w, enc_node_w, proc_edge_w,
         proc_node_w, mesh_nodes, mesh_edge,
-        enc_patch.reshape(1, edges), enc_sender.reshape(1, edges), enc_node.reshape(1, edges),
+        enc_patch.reshape(1, edges), enc_sender, enc_node,
         enc_geo, mesh_send.reshape(1, medges), mesh_recv.reshape(1, medges), halo_rows,
     )
 

time: 138 us -> 99 us (0.72)
  Pallas kernels: 128 us -> 96.6 us
  local copies, waits for them, and re-layouts: 7.68 us -> 1.43 us
    pallas_call x1, Pallas kernels: 128 us -> 96.6 us  [per_device(): pl.pallas_call(functools.partial(kernel, nb, np_, ny), out_shape=(pltpu.V...]
    unnamed x3 -> x2, local copies, waits for them, and re-layouts: 5.17 us -> 1.43 us
    reshape x2 -> x0, local copies, waits for them, and re-layouts: 2.5 us -> none  [the longest x1 1.26 us: per_device(): enc_node.reshape(1, edges)]
where the time goes in v3:
time: 99 us; the launch traced here: 98.7 us
  Pallas kernels  96.6 us (98%)
  local copies, waits for them, and re-layouts  1.43 us (1%)
    pallas_call x1, Pallas kernels, per_device(): pl.pallas_call(functools.partial(kernel, nb, np_, ny), out_shape=(pltpu.V...  96.6 us

profile of v3, /device:TPU:6, one launch (start us, length us, event | category | flops | bytes accessed | tf_op | source)
XLA Modules:
  0.0 98.7 jit_solution(15727932426449700442)
XLA Ops:
  0.6 96.6 %shard_map.176 = (bf16[320,512]{1,0:T(8,128)(2,1)S(1)}, bf16[256,512]{1,0:T(8,128)(2,1)S(1)}) custom-call(bf16[474,256]{1,0:T(8,128)(2,1)} %bitcast.4, bf16[474,512]{1,0:T(8,128)(2,1)} %gi_h.1, bf16[512,512]{1,0:T(8,128)(2,1)} %go_h.1, bf16[4,512]{1,0:T(4,128)(2,1)} %gw.1, bf16[3,512,512]{2,1,0:T(8,128)(2,1)} %ee_h.1, bf16[3,512,512]{2,1,0:T(8,128)(2,1)} %en_h.1, ...), custom_call_target="tpu_custom_call" | custom-call | tf_op jit(solution)/shard_map/pallas_call | solution.py:361
  97.3 0.7 copy.21
  98.0 0.7 copy.22

commit v4 on v3

--- a/solution.py
+++ b/solution.py
@@ -57,7 +57,7 @@
     addr_out, addr_in, outbox, inbox, rs_out, rs_in, ag_out, ag_in,
     halo_out, halo_in, rs2_out, rs2_in, ag2_out, ag2_in,
     via_in, via_out, via2_in, via2_out, left_pick, right_pick,
-    recv_proj, edge_proj, one_ref, placed, total, ssem, rsem,
+    recv_proj, edge_proj, one_ref, placed, total, grid_pick, geo_pick, ssem, rsem,
 ):
     b = lax.axis_index("band")
     p = lax.axis_index("patch")
@@ -109,20 +109,32 @@
     def greet(axis, q):
         pl.semaphore_signal(barrier, inc=1, device_id={axis: q}, device_id_type=MESH)
 
+    for k in range(nb // 2, 0, -1):
+        greet("band", (b + k) % nb)
+        if 2 * k != nb:
+            greet("band", (b + nb - k) % nb)
     each_peer(lambda q, dx: greet("patch", q))
-    for k in range(1, nb):
-        greet("band", (b + k) % nb)
-
-    def to_patches(src, dst, send, recv, apart):
+
+    def to_patches(src, dst, send, recv):
         def visit(q, dx):
             pltpu.make_async_remote_copy(
                 src_ref=src.at[q], dst_ref=dst.at[p], send_sem=ssem.at[send],
-                recv_sem=rsem.at[recv + dx if apart else recv],
+                recv_sem=rsem.at[recv],
                 device_id={"patch": q}, device_id_type=MESH,
             ).start()
 
         each_peer(visit)
         dst[p] = src[p]
+
+    def to_column(src, dst, send, recv, dx):
+        first = (x0 + dx) % nx * per
+        for where, spot in spots:
+            if dx or where != (0, 0):
+                q = first + spot
+                pltpu.make_async_remote_copy(
+                    src_ref=src.at[q], dst_ref=dst.at[p], send_sem=ssem.at[send],
+                    recv_sem=rsem.at[recv + dx], device_id={"patch": q}, device_id_type=MESH,
+                ).start()
 
     sides = ((0, 1, pl.ds(0, cut)), (1, -1, pl.ds(cut, block - cut)))
 
@@ -205,12 +217,22 @@
     latent = norm_rows(mm(hidden, go[...])).astype(BF16)
     loads[3].wait()
     sender_proj = mm(latent, ee[0]).astype(BF16)
-    terms = mm(from_grid, sender_proj) + mm(geo_rows, gw[...])
-    outbox[...] = terms.reshape(np_, CAP, width).astype(BF16)
-
+    grid_pick[...] = from_grid
+    geo_pick[...] = geo_rows
+
+    def fill(x):
+        rows = pl.ds(x * (per * CAP), per * CAP)
+        terms = mm(grid_pick[rows], sender_proj) + mm(geo_pick[rows], gw[...])
+        outbox[pl.ds(x * per, per)] = terms.reshape(per, CAP, width).astype(BF16)
+
+    fill(x0)
     pl.semaphore_wait(barrier, np_ + nb - 2)
-    to_patches(addr_out, addr_in, 0, 0, False)
-    to_patches(outbox, inbox, 1, 19, True)
+    to_patches(addr_out, addr_in, 0, 0)
+    to_column(outbox, inbox, 1, 19, 0)
+    for dx in range(1, nx):
+        fill((x0 + dx) % nx)
+        to_column(outbox, inbox, 1, 19, dx)
+    inbox[p] = outbox[p]
 
     loads[4].wait()
     recv_proj[...] = mm(mn[...], ee[1]).astype(BF16)
@@ -312,7 +334,7 @@
     going = mm_cols(halo_pick, sent)
     going = jnp.where(left_slots, going[:, :half], going[:, half:])
     halo_out[...] = going.reshape(np_, CAP, half).astype(BF16)
-    to_patches(halo_out, halo_in, 4, 4, False)
+    to_patches(halo_out, halo_in, 4, 4)
     recv_two = mm(one_ref[...], pe[2]).astype(BF16)
     edge_proj[...] += mm_cols(local_pick, sent) + mm_cols(recv_pick, recv_two)
 
@@ -383,6 +405,7 @@
             pltpu.VMEM((count, width), BF16), pltpu.VMEM((medges, width), F32),
             pltpu.VMEM((count, width), BF16),
             pltpu.VMEM((np_ // (2 * ny), 1, 128), F32), pltpu.VMEM((2 * count, width), F32),
+            pltpu.VMEM((slots, grid_feat.shape[0]), BF16), pltpu.VMEM((slots, 4), BF16),
             pltpu.SemaphoreType.DMA((7,)), pltpu.SemaphoreType.DMA((23 + np_ // (2 * ny),)),
         ],
         compiler_params=pltpu.CompilerParams(collective_id=0, has_side_effects=True),

time: 99 us -> 99.5 us (level)
  no operation moved by 1% of the time
where the time goes in v4:
time: 99.5 us; the launch traced here: 98.9 us
  Pallas kernels  96.8 us (97%)
  local copies, waits for them, and re-layouts  1.43 us (1%)
    pallas_call x1, Pallas kernels, per_device(): pl.pallas_call(functools.partial(kernel, nb, np_, ny), out_shape=(pltpu.V...  96.8 us

profile of v4, /device:TPU:6, one launch (start us, length us, event | category | flops | bytes accessed | tf_op | source)
XLA Modules:
  0.0 98.9 jit_solution(10786783856474226054)
XLA Ops:
  0.6 96.8 %shard_map.176 = (bf16[320,512]{1,0:T(8,128)(2,1)S(1)}, bf16[256,512]{1,0:T(8,128)(2,1)S(1)}) custom-call(bf16[474,256]{1,0:T(8,128)(2,1)} %bitcast.4, bf16[474,512]{1,0:T(8,128)(2,1)} %gi_h.1, bf16[512,512]{1,0:T(8,128)(2,1)} %go_h.1, bf16[4,512]{1,0:T(4,128)(2,1)} %gw.1, bf16[3,512,512]{2,1,0:T(8,128)(2,1)} %ee_h.1, bf16[3,512,512]{2,1,0:T(8,128)(2,1)} %en_h.1, ...), custom_call_target="tpu_custom_call" | custom-call | tf_op jit(solution)/shard_map/pallas_call | solution.py:383
  97.5 0.7 copy.21
  98.2 0.7 copy.22
